TPU v7x, 512 devices: a whole 4x4x16 slice. The times are simulated.
512 devices in a mesh: section: 2 (over y_lo), grp: 32 (over z, core), tp: 8 (over x, y_hi).
Axes of the slice: x: 4, y: 4 (y_hi: 2, y_lo: 2; y = y_hi * 2 + y_lo), z: 16, core: 2. Of those that a mesh axis runs over, the one named last changes fastest.
Arguments:
- partials: bfloat16 [8, 2, 4096, 8192], P('tp', 'section', 'grp'), may hold values from -3 to 3
- residual: bfloat16 [2, 4096, 8192], P('section', 'grp', 'tp'), may hold values from -300 to 300
- norm_gain: bfloat16 [8192], replicated, may hold values from 0.099609375 to 1.8984375
- w_query: bfloat16 [8192, 8192], P('grp', ('section', 'tp')), may hold values from -0.0625 to 0.0625
- w_keyval: bfloat16 [8192, 2048], P('grp', ('section', 'tp')), may hold values from -0.0625 to 0.0625
- bias_query: bfloat16 [8192], P(('section', 'tp')), may hold values from -3 to 3
- bias_keyval: bfloat16 [2048], P(('section', 'tp')), may hold values from -3 to 3
Outputs:
- hidden: bfloat16 [2, 4096, 8192], P('section', 'grp', 'tp')
- query: bfloat16 [2, 4096, 8192], P(None, 'grp', ('section', 'tp'))
- keyval: bfloat16 [2, 4096, 2048], P(None, 'grp', ('section', 'tp'))
All inputs are finite; a program needn't handle non-finite values.
Results may differ from a plain program's by a relative error of at most 0.01.
Values may be sent and summed in bfloat16 or wider, within the bound.
No kernel may reach another device: no remote copies, remote signals or barrier semaphores. Data moves between devices by JAX's collectives and lax.ppermute only.
A program may use at most 64 MiB of HBM per device.

v0:
```python
import jax
import jax.numpy as jnp
from jax import lax
from jax.sharding import PartitionSpec as P

epsilon = 1e-06


def laid_out(parts, dim):
    dims = list(parts.shape[1:])
    dims[dim] *= parts.shape[0]
    return jnp.moveaxis(parts, 0, dim).reshape(dims)


def sent_to_all(value, axis):
    copies = jnp.broadcast_to(value, (lax.axis_size(axis), *value.shape))
    return lax.all_to_all(copies, axis, split_axis=0, concat_axis=0, tiled=True)


def gathered_copies(value, axis, dim):
    return laid_out(sent_to_all(value, axis), dim)


def cut_along(value, dim, peers):
    dims = value.shape
    parts = value.reshape(*dims[:dim], peers, dims[dim] // peers, *dims[dim + 1 :])
    return jnp.moveaxis(parts, dim, 0)


def sent_and_summed(value, axis, dim):
    parts = cut_along(value, dim, lax.axis_size(axis))
    arrived = lax.all_to_all(parts, axis, split_axis=0, concat_axis=0, tiled=True)
    return arrived.astype(jnp.float32).sum(axis=0)


def taken_together(value, axis):
    return sent_to_all(value, axis).sum(axis=0)


def in_one_piece(arrays, axis, dim, along):
    both = jnp.concatenate(arrays, axis=along)
    filled, at, gathered = (lax.all_gather(both, axis, axis=dim, tiled=True), 0, [])
    for a in arrays:
        gathered.append(lax.slice_in_dim(filled, at, at + a.shape[along], axis=along))
        at += a.shape[along]
    return tuple(gathered)


def spread_tp(normed):
    return gathered_copies(normed, "tp", 2)


def local(partials, residual, norm_gain, w_query, w_keyval, bias_query, bias_keyval):
    model_width = norm_gain.shape[0]
    partial_term = partials[0].astype(jnp.float32)
    scaled_gain = norm_gain.astype(jnp.float32)
    summed = sent_and_summed(partial_term.astype(jnp.bfloat16), "tp", 2)
    hidden = (residual.astype(jnp.float32) + summed).astype(jnp.bfloat16)
    widened = hidden.astype(jnp.float32)
    squares = taken_together(jnp.sum(widened * widened, axis=-1), "tp")
    feature_share = widened.shape[2]
    offset = lax.axis_index("tp") * feature_share
    local_gain = lax.dynamic_slice_in_dim(scaled_gain, offset, feature_share, 0)
    mean_square = squares[..., None] / model_width
    normed = (widened * lax.rsqrt(mean_square + epsilon) * local_gain).astype(jnp.bfloat16)
    gathered = spread_tp(gathered_copies(normed, "section", 0))
    flattened = gathered.reshape(-1, model_width)
    pieces = in_one_piece((w_query, w_keyval), "grp", 0, 1)
    query_total = jnp.dot(flattened, pieces[0], preferred_element_type=jnp.float32)
    keyval_total = jnp.dot(flattened, pieces[1], preferred_element_type=jnp.float32)
    query = (query_total + bias_query.astype(jnp.float32)).astype(jnp.bfloat16)
    keyval = (keyval_total + bias_keyval.astype(jnp.float32)).astype(jnp.bfloat16)
    query = query.reshape(gathered.shape[0], gathered.shape[1], -1)
    keyval = keyval.reshape(gathered.shape[0], gathered.shape[1], -1)
    return (hidden, query, keyval)


def solution(mesh):
    placed = (
        P("tp", "section", "grp", None),
        P("section", "grp", "tp"),
        P(),
        P("grp", ("section", "tp")),
        P("grp", ("section", "tp")),
        P(("section", "tp")),
        P(("section", "tp")),
    )
    return jax.shard_map(
        local,
        mesh=mesh,
        in_specs=placed,
        out_specs=(
            P("section", "grp", "tp"),
            P(None, "grp", ("section", "tp")),
            P(None, "grp", ("section", "tp")),
        ),
        check_vma=False,
    )
```

profile of v0, /device:TPU:480, one launch (start us, length us, event | category | flops | bytes accessed | tf_op | source)
XLA Modules:
  0.0 167.9 jit_solution(13051668522855743631)
XLA Ops:
  7.2 0.0 all-gather.2.cloned.1.call-start
  7.2 1.8 %pad_maximum_fusion = bf16[256,640]{1,0:T(8,128)(2,1)} fusion(bf16[256,128]{1,0:T(8,128)(2,1)} %param.11, bf16[256,512]{1,0:T(8,128)(2,1)} %param.10), kind=kLoop, calls=%fused_computation.16 | loop fusion | flops 655360 | bytes 655360 | tf_op jit(solution)/shard_map/concatenate | solution.py:41
  9.0 0.0 all-gather.2.cloned.1.call-update
  9.0 3.2 %copy.17 = bf16[1,1,128,8192]{2,3,1,0:T(8,128)(2,1)S(1)} copy(bf16[1,1,128,8192]{3,2,1,0:T(8,128)(2,1)} %param.7) | data formatting | bytes 4194304 | tf_op args[0]
  12.2 2.6 %copy.18 = bf16[8,1,128,1024]{3,2,1,0:T(8,128)(2,1)} copy(bf16[8,1,128,1024]{2,3,0,1:T(8,128)(2,1)S(1)} %bitcast.21) | data formatting | bytes 4194304 | tf_op jit(solution)/shard_map/transpose | solution.py:27
  14.8 0.0 copy-start.2
  14.8 7.1 %all-to-all-start = ((bf16[8,1,128,1024]{3,2,1,0:T(8,128)(2,1)}), bf16[8,1,128,1024]{3,2,1,0:T(8,128)(2,1)S(1)}, u32[]{:S(2)}, u32[]{:S(2)}) async-start(bf16[8,1,128,1024]{3,2,1,0:T(8,128)(2,1)} %copy.18), calls=%async_computation | async-start | bytes 4194304 | tf_op jit(solution)/shard_map/all_to_all | solution.py:32
  21.9 31.2 %all-to-all-done = bf16[8,1,128,1024]{3,2,1,0:T(8,128)(2,1)S(1)} async-done(((bf16[8,1,128,1024]{3,2,1,0:T(8,128)(2,1)}), bf16[8,1,128,1024]{3,2,1,0:T(8,128)(2,1)S(1)}, u32[]{:S(2)}, u32[]{:S(2)}) %all-to-all-start) | async-done | bytes 2097184 | tf_op jit(solution)/shard_map/all_to_all | solution.py:32
  53.1 0.3 convert_reduce_fusion
  53.5 0.0 copy-done.2
  53.5 0.2 fusion.16
  53.7 0.0 copy-start.1
  53.7 0.6 broadcast_in_dim.6
  54.3 3.3 %all-to-all-start.1 = ((f32[8,1,128]{2,1,0:T(1,128)}), f32[8,1,128]{2,1,0:T(1,128)S(1)}, u32[]{:S(2)}, u32[]{:S(2)}) async-start(f32[8,1,128]{2,1,0:T(1,128)} %broadcast_in_dim.6), calls=%async_computation.1 | async-start | bytes 8192 | tf_op jit(solution)/shard_map/all_to_all | solution.py:17
  57.6 0.7 dynamic-slice_convert_fusion
  58.3 6.8 %all-to-all-done.1 = f32[8,1,128]{2,1,0:T(1,128)S(1)} async-done(((f32[8,1,128]{2,1,0:T(1,128)}), f32[8,1,128]{2,1,0:T(1,128)S(1)}, u32[]{:S(2)}, u32[]{:S(2)}) %all-to-all-start.1) | async-done | bytes 4128 | tf_op jit(solution)/shard_map/all_to_all | solution.py:17
  65.2 0.1 fusion.20
  65.3 0.1 broadcast_in_dim.14
  65.4 9.0 %all_to_all.20 = bf16[2,1,128,1024]{3,2,1,0:T(8,128)(2,1)S(1)} all-to-all(bf16[2,1,128,1024]{3,2,1,0:T(8,128)(2,1)S(1)} %broadcast_in_dim.14), channel_id=1, replica_groups=mesh['section'=2,'grp'=32,'tp'=8] {'section'}, dimensions={0} | all-to-all | bytes 1048576 | tf_op jit(solution)/shard_map/all_to_all | solution.py:17
  74.4 2.5 %broadcast_in_dim.15 = bf16[8,2,128,1024]{3,2,1,0:T(8,128)(2,1)} broadcast(bf16[2,128,1024]{2,1,0:T(8,128)(2,1)S(1)} %bitcast.24), dimensions={1,2,3} | broadcast | bytes 4718592 | tf_op jit(solution)/shard_map/broadcast_in_dim | solution.py:16
  76.9 0.0 copy-start.3
  76.9 0.0 copy-start.4
  76.9 0.0 copy-done.1
  76.9 4.9 %all-to-all-start.3 = ((bf16[8,2,128,1024]{3,2,1,0:T(8,128)(2,1)}), bf16[8,2,128,1024]{3,2,1,0:T(8,128)(2,1)}, u32[]{:S(2)}, u32[]{:S(2)}) async-start(bf16[8,2,128,1024]{3,2,1,0:T(8,128)(2,1)} %broadcast_in_dim.15), calls=%async_computation.3 | async-start | bytes 8388608 | tf_op jit(solution)/shard_map/all_to_all | solution.py:17
  81.8 0.0 copy-done.3
  81.8 0.0 copy-done.4
  81.9 57.0 %all-to-all-done.3 = bf16[8,2,128,1024]{3,2,1,0:T(8,128)(2,1)} async-done(((bf16[8,2,128,1024]{3,2,1,0:T(8,128)(2,1)}), bf16[8,2,128,1024]{3,2,1,0:T(8,128)(2,1)}, u32[]{:S(2)}, u32[]{:S(2)}) %all-to-all-start.3) | async-done | bytes 4194336 | tf_op jit(solution)/shard_map/all_to_all | solution.py:17
  138.8 4.5 %copy.20 = bf16[2,128,8,1024]{3,2,1,0:T(8,128)(2,1)S(1)} copy(bf16[2,128,8,1024]{3,1,0,2:T(8,128)(2,1)} %bitcast.6) | data formatting | bytes 8388608 | tf_op jit(solution)/shard_map/transpose | solution.py:12
  143.3 6.4 %copy.21 = bf16[32,8,8,1024]{3,1,2,0:T(8,128)(2,1)} copy(bf16[32,8,8,1024]{3,2,1,0:T(8,128)(2,1)S(1)} %bitcast.20) | data formatting | bytes 8388608
  149.7 0.0 all-gather.2.cloned.1.call-done
  149.7 0.0 copy-start
  149.7 7.8 %fusion.7 = bf16[256,512]{1,0:T(8,128)(2,1)} fusion(bf16[256,8192]{1,0:T(8,128)(2,1)} %bitcast.22, bf16[8192,640]{1,0:T(8,128)(2,1)} %all-gather.2.cloned.1.call-done, f32[512]{0:T(512)S(1)} %convert_element_type.41), kind=kOutput, calls=%fused_computation.6 | convolution fusion | flops 2147745792 | bytes 12847104 | tf_op jit(solution)/shard_map/dot_general | solution.py:69
  157.6 0.0 copy-done
  157.6 3.5 %fusion.13 = bf16[256,128]{1,0:T(8,128)(2,1)} fusion(bf16[256,8192]{1,0:T(8,128)(2,1)S(1)} %bitcast.23, bf16[8192,640]{1,0:T(8,128)(2,1)} %all-gather.2.cloned.1.call-done, f32[128]{0:T(128)S(1)} %convert_element_type.43), kind=kOutput, calls=%fused_computation.8 | convolution fusion | flops 536936448 | bytes 6357504 | tf_op jit(solution)/shard_map/dot_general | solution.py:70
  (4 shorter events, 0.0 us)
Async XLA Ops:
  7.2 142.6 %all-gather.2.cloned.1.call-start = ((), (), s32[]{:S(2)}) async-start(), calls=%async_computation.4 | async-start | bytes 10813440 | tf_op jit(solution)/shard_map/all_gather | solution.py:42
  14.8 38.6 %copy-start.2 = (bf16[1,128,1024]{2,1,0:T(8,128)(2,1)S(1)}, bf16[1,128,1024]{2,1,0:T(8,128)(2,1)}, u32[]{:S(2)}) copy-start(bf16[1,128,1024]{2,1,0:T(8,128)(2,1)} %param.8) | copy-start | bytes 786436
  14.8 38.3 %all-to-all-start = ((bf16[8,1,128,1024]{3,2,1,0:T(8,128)(2,1)}), bf16[8,1,128,1024]{3,2,1,0:T(8,128)(2,1)S(1)}, u32[]{:S(2)}, u32[]{:S(2)}) async-start(bf16[8,1,128,1024]{3,2,1,0:T(8,128)(2,1)} %copy.18), calls=%async_computation | async-start | bytes 4194304 | tf_op jit(solution)/shard_map/all_to_all | solution.py:32
  53.7 23.2 %copy-start.1 = (bf16[1,128,1024]{2,1,0:T(8,128)(2,1)}, bf16[1,128,1024]{2,1,0:T(8,128)(2,1)S(1)}, u32[]{:S(2)}) copy-start(bf16[1,128,1024]{2,1,0:T(8,128)(2,1)S(1)} %get-tuple-element.4) | copy-start | bytes 786436
  54.3 10.8 %all-to-all-start.1 = ((f32[8,1,128]{2,1,0:T(1,128)}), f32[8,1,128]{2,1,0:T(1,128)S(1)}, u32[]{:S(2)}, u32[]{:S(2)}) async-start(f32[8,1,128]{2,1,0:T(1,128)} %broadcast_in_dim.6), calls=%async_computation.1 | async-start | bytes 8192 | tf_op jit(solution)/shard_map/all_to_all | solution.py:17
  76.9 4.9 %copy-start.3 = (bf16[512]{0:T(512)(128)(2,1)S(1)}, bf16[512]{0:T(512)(128)(2,1)}, u32[]{:S(2)}) copy-start(bf16[512]{0:T(512)(128)(2,1)} %param.12) | copy-start | bytes 3076
  76.9 5.0 %copy-start.4 = (bf16[128]{0:T(256)(128)(2,1)S(1)}, bf16[128]{0:T(256)(128)(2,1)}, u32[]{:S(2)}) copy-start(bf16[128]{0:T(256)(128)(2,1)} %param.13) | copy-start | bytes 772
  76.9 61.9 %all-to-all-start.3 = ((bf16[8,2,128,1024]{3,2,1,0:T(8,128)(2,1)}), bf16[8,2,128,1024]{3,2,1,0:T(8,128)(2,1)}, u32[]{:S(2)}, u32[]{:S(2)}) async-start(bf16[8,2,128,1024]{3,2,1,0:T(8,128)(2,1)} %broadcast_in_dim.15), calls=%async_computation.3 | async-start | bytes 8388608 | tf_op jit(solution)/shard_map/all_to_all | solution.py:17
  149.7 7.8 %copy-start = (bf16[32,8,8,1024]{3,1,2,0:T(8,128)(2,1)S(1)}, bf16[32,8,8,1024]{3,1,2,0:T(8,128)(2,1)}, u32[]{:S(2)}) copy-start(bf16[32,8,8,1024]{3,1,2,0:T(8,128)(2,1)} %copy.21) | copy-start | bytes 12582916
Sparse Core Ops, SparseCore 0:
  10.1 78.3 all-gather.1
where the time goes:
time: 168 us
  waiting for transfers between devices  95.1 us (57%)
  local copies, waits for them, and re-layouts  20 us (12%)
  starting transfers between devices  15.3 us (9%)
  between operations  14.1 us (8%)
  matrix products  11.3 us (7%)
  blocking collectives  8.99 us (5%)
  other arithmetic  3.12 us (2%)
    all_to_all x2, waiting for transfers between devices, sent_to_all(): return lax.all_to_all(copies, axis, split_axis=0, concat_axis=0, tiled=True)  63.8 us
    all_to_all x1, waiting for transfers between devices, sent_and_summed(): lax.all_to_all(parts, axis, split_axis=0, concat_axis=0, tiled=True)  31.2 us
    unnamed x12, local copies, waits for them, and re-layouts  9.64 us
    all_to_all x1, blocking collectives, sent_to_all(): return lax.all_to_all(copies, axis, split_axis=0, concat_axis=0, tiled=True)  8.99 us
    all_to_all x2, starting transfers between devices, sent_to_all(): return lax.all_to_all(copies, axis, split_axis=0, concat_axis=0, tiled=True)  8.23 us
    dot_general x1, matrix products, local(): jnp.dot(flattened, pieces[0], preferred_element_type=jnp.float32)  7.82 us
    all_to_all x1, starting transfers between devices, sent_and_summed(): lax.all_to_all(parts, axis, split_axis=0, concat_axis=0, tiled=True)  7.06 us
    transpose x1, local copies, waits for them, and re-layouts, laid_out(): return jnp.moveaxis(parts, 0, dim).reshape(dims)  4.51 us
  transfers between devices with their start and end apart: 4, of which 3 were waited for; matrix products, arithmetic and copies ran while one was open for 13% of the time, Pallas kernels for 0%

commit v1 on v0

v1 whole, which is shorter than its diff:
```python
import jax
import jax.numpy as jnp
from jax import lax
from jax.experimental import pallas as pl
from jax.experimental.pallas import tpu as pltpu
from jax.sharding import PartitionSpec as P

epsilon = 1e-06
MESH_AXES = ("section", "grp", "tp")


def plane_groups(mesh, along_x_core):
    n_sec, n_grp, n_tp = (mesh.shape[a] for a in MESH_AXES)

    def device(x, y, g):
        y_hi, y_lo = divmod(y, n_sec)
        return (y_lo * n_grp + g) * n_tp + x * 2 + y_hi

    n_x, n_y = n_tp // 2, 2 * n_sec
    groups = []
    for g in range(n_grp):
        if g % 2 == along_x_core:
            groups += [[device(x, y, g) for x in range(n_x)] for y in range(n_y)]
        else:
            groups += [[device(x, y, g) for y in range(n_y)] for x in range(n_x)]
    return groups


def copy_body(src, dst):
    dst[0] = src[...]


def blocks_of_features(partial, blocks):
    rows, width = partial.shape
    share = width // blocks
    return pl.pallas_call(
        copy_body,
        grid=(blocks,),
        in_specs=[pl.BlockSpec((rows, share), lambda i: (0, i))],
        out_specs=pl.BlockSpec((1, rows, share), lambda i: (i, 0, 0)),
        out_shape=jax.ShapeDtypeStruct((blocks, rows, share), partial.dtype),
        name="cut_features",
    )(partial)


def project_body(table, first, second, gain, weights, bias, query, keyval, total, squares):
    step = pl.program_id(0)
    rows = first.shape[1]

    @pl.when(step == 0)
    def _():
        total[...] = jnp.zeros_like(total)
        squares[...] = jnp.zeros_like(squares)

    scale = gain[0].astype(jnp.float32)
    for s, block in enumerate((first, second)):
        at = pl.ds(s * rows, rows)
        hidden = block[0].astype(jnp.float32)
        squares[at, :] += jnp.sum(hidden * hidden, axis=-1, keepdims=True)
        scaled = (hidden * scale).astype(jnp.bfloat16)
        total[at, :] += jnp.dot(scaled, weights[...], preferred_element_type=jnp.float32)

    @pl.when(step == pl.num_programs(0) - 1)
    def _():
        width = pl.num_programs(0) * first.shape[2]
        root = lax.rsqrt(squares[...] / width + epsilon)
        result = total[...] * root + bias[...].astype(jnp.float32)
        split = query.shape[2]
        for s in range(2):
            at = slice(s * rows, (s + 1) * rows)
            query[s] = result[at, :split].astype(query.dtype)
            keyval[s] = result[at, split:].astype(keyval.dtype)


def project(table, gathered, gain, weights, bias, query_width):
    _, rows, share = gathered.shape
    width, cols = weights.shape
    steps = width // share
    block = (1, rows, share)
    return pl.pallas_call(
        project_body,
        grid_spec=pltpu.PrefetchScalarGridSpec(
            num_scalar_prefetch=1,
            grid=(steps,),
            in_specs=[
                pl.BlockSpec(block, lambda k, t: (t[0, k], 0, 0)),
                pl.BlockSpec(block, lambda k, t: (t[1, k], 0, 0)),
                pl.BlockSpec((1, 1, share), lambda k, t: (k, 0, 0)),
                pl.BlockSpec((share, cols), lambda k, t: (k, 0)),
                pl.BlockSpec((1, cols), lambda k, t: (0, 0)),
            ],
            out_specs=[
                pl.BlockSpec((2, rows, query_width), lambda k, t: (0, 0, 0)),
                pl.BlockSpec((2, rows, cols - query_width), lambda k, t: (0, 0, 0)),
            ],
            scratch_shapes=[
                pltpu.VMEM((2 * rows, cols), jnp.float32),
                pltpu.VMEM((2 * rows, 1), jnp.float32),
            ],
        ),
        out_shape=[
            jax.ShapeDtypeStruct((2, rows, query_width), jnp.bfloat16),
            jax.ShapeDtypeStruct((2, rows, cols - query_width), jnp.bfloat16),
        ],
        name="project",
    )(table, gathered, gathered, gain.reshape(steps, 1, share), weights, bias)


def spread(value, groups):
    copies = jnp.broadcast_to(value, (4, *value.shape))
    return lax.all_to_all(copies, MESH_AXES, split_axis=0, concat_axis=0, tiled=True, axis_index_groups=groups)


def solution(mesh):
    first_groups = plane_groups(mesh, 1)
    second_groups = plane_groups(mesh, 0)

    def local(partials, residual, norm_gain, w_query, w_keyval, bias_query, bias_keyval):
        weights = lax.all_gather(jnp.concatenate([w_query, w_keyval], axis=1), "grp", axis=0, tiled=True)
        n_tp = lax.axis_size("tp")
        parts = blocks_of_features(partials[0, 0], n_tp)
        arrived = lax.all_to_all(parts, "tp", split_axis=0, concat_axis=0, tiled=True)
        summed = arrived.astype(jnp.float32).sum(axis=0)
        hidden = (residual[0].astype(jnp.float32) + summed).astype(jnp.bfloat16)
        gathered = spread(spread(hidden, first_groups), second_groups)
        gathered = gathered.reshape(16, *hidden.shape)
        core = lax.axis_index("grp") % 2
        section = jnp.arange(2)[:, None]
        part = jnp.arange(n_tp)[None, :]
        along_y = part * 2 + section
        along_x = (part % 2) * 8 + section * 4 + part // 2
        table = jnp.where(core == 0, along_y, along_x).astype(jnp.int32)
        bias = jnp.concatenate([bias_query, bias_keyval])[None, :]
        query, keyval = project(table, gathered, norm_gain, weights, bias, w_query.shape[1])
        return hidden[None], query, keyval

    placed = (
        P("tp", "section", "grp", None),
        P("section", "grp", "tp"),
        P(),
        P("grp", ("section", "tp")),
        P("grp", ("section", "tp")),
        P(("section", "tp")),
        P(("section", "tp")),
    )
    return jax.shard_map(
        local,
        mesh=mesh,
        in_specs=placed,
        out_specs=(
            P("section", "grp", "tp"),
            P(None, "grp", ("section", "tp")),
            P(None, "grp", ("section", "tp")),
        ),
        check_vma=False,
    )
```

time: 168 us -> 118 us (0.70)
  waiting for transfers between devices: 95.1 us -> 25.2 us
  blocking collectives: 8.99 us -> 48.6 us
  Pallas kernels: 0 us -> 16.7 us
  local copies, waits for them, and re-layouts: 20 us -> 3.9 us
  matrix products: 11.3 us -> 0 us
  starting transfers between devices: 15.3 us -> 5.04 us
    all_to_all x3 -> x1, waiting for transfers between devices: 95 us -> 25.1 us  [spread(): lax.all_to_all(copies, MESH_AXES, split_axis=0, concat_axis=0, tiled=True...]
    all_to_all x1 -> x2, blocking collectives: 8.99 us -> 48.6 us  [the longest x1 35.1 us: local(): lax.all_to_all(parts, 'tp', split_axis=0, concat_axis=0, tiled=True)]
    pallas_call x0 -> x2, Pallas kernels: none -> 16.7 us  [the longest x1 11 us: project(): pl.pallas_call(project_body, grid_spec=pltpu.PrefetchScalarGridSpec(num_s...]
    dot_general x2 -> x0, matrix products: 11.3 us -> none  [the longest x1 7.82 us: local(): jnp.dot(flattened, pieces[0], preferred_element_type=jnp.float32)]
    all_to_all x3 -> x1, starting transfers between devices: 15.3 us -> 5 us  [spread(): lax.all_to_all(copies, MESH_AXES, split_axis=0, concat_axis=0, tiled=True...]
    unnamed x12 -> x8, local copies, waits for them, and re-layouts: 9.64 us -> 0.01 us
    transpose x2 -> x0, local copies, waits for them, and re-layouts: 7.13 us -> none  [the longest x1 4.51 us: laid_out(): return jnp.moveaxis(parts, 0, dim).reshape(dims)]
  transfers between devices with their start and end apart: 4 -> 2, of which waited for: 3 -> 1; matrix products, arithmetic and copies ran while one was open for 13% -> 5% of each run, Pallas kernels for 0% -> 5%
where the time goes in v1:
time: 118 us; the launch traced here: 117 us
  blocking collectives  48.6 us (41%)
  waiting for transfers between devices  25.2 us (21%)
  Pallas kernels  16.7 us (14%)
  between operations  14.1 us (12%)
  starting transfers between devices  5.04 us (4%)
  local copies, waits for them, and re-layouts  3.9 us (3%)
  other arithmetic  3.57 us (3%)
    all_to_all x1, blocking collectives, local(): lax.all_to_all(parts, 'tp', split_axis=0, concat_axis=0, tiled=True)  35.1 us
    all_to_all x1, waiting for transfers between devices, spread(): lax.all_to_all(copies, MESH_AXES, split_axis=0, concat_axis=0, tiled=True...  25.1 us
    all_to_all x1, blocking collectives, spread(): lax.all_to_all(copies, MESH_AXES, split_axis=0, concat_axis=0, tiled=True...  13.5 us
    pallas_call x1, Pallas kernels, project(): pl.pallas_call(project_body, grid_spec=pltpu.PrefetchScalarGridSpec(num_s...  11 us
    pallas_call x1, Pallas kernels, blocks_of_features(): pl.pallas_call(copy_body, grid=(blocks,), in_specs=[pl.BlockSpec((rows, s...  5.65 us
    all_to_all x1, starting transfers between devices, spread(): lax.all_to_all(copies, MESH_AXES, split_axis=0, concat_axis=0, tiled=True...  5 us
    broadcast_in_dim x2, local copies, waits for them, and re-layouts, spread(): copies = jnp.broadcast_to(value, (4, *value.shape))  2.68 us
  transfers between devices with their start and end apart: 2, of which 1 were waited for; matrix products, arithmetic and copies ran while one was open for 5% of the time, Pallas kernels for 5%

profile of v1, /device:TPU:480, one launch (start us, length us, event | category | flops | bytes accessed | tf_op | source)
XLA Modules:
  0.0 117.1 jit_solution(6230472306955126609)
XLA Ops:
  7.2 0.0 all-gather.2.cloned.1.call-start
  7.2 1.7 %pad_maximum_fusion = bf16[256,640]{1,0:T(8,128)(2,1)} fusion(bf16[256,128]{1,0:T(8,128)(2,1)} %param.11, bf16[256,512]{1,0:T(8,128)(2,1)} %param.10), kind=kLoop, calls=%fused_computation.6 | loop fusion | flops 655360 | bytes 655360 | tf_op jit(solution)/shard_map/concatenate | solution.py:119
  8.9 0.0 all-gather.2.cloned.1.call-update
  9.0 5.6 %cut_features.1 = bf16[8,128,1024]{2,1,0:T(8,128)(2,1)} custom-call(bf16[128,8192]{1,0:T(8,128)(2,1)} %bitcast.10), custom_call_target="tpu_custom_call" | custom-call | tf_op jit(solution)/shard_map/cut_features/pallas_call | solution.py:36
  14.6 0.0 copy-start
  14.6 35.1 %all_to_all.15 = bf16[8,128,1024]{2,1,0:T(8,128)(2,1)S(1)} all-to-all(bf16[8,128,1024]{2,1,0:T(8,128)(2,1)} %cut_features.1), channel_id=1, replica_groups=mesh['section'=2,'grp'=32,'tp'=8] {'tp'}, dimensions={0} | all-to-all | bytes 4194304 | tf_op jit(solution)/shard_map/all_to_all | solution.py:122
  49.8 0.4 convert_reduce_fusion
  50.1 0.0 copy-done
  50.1 0.1 fusion.2
  50.2 0.1 broadcast_in_dim.12
  50.3 13.5 %all_to_all.16 = bf16[4,128,1024]{2,1,0:T(8,128)(2,1)S(1)} all-to-all(bf16[4,128,1024]{2,1,0:T(8,128)(2,1)S(1)} %broadcast_in_dim.12), channel_id=1, replica_groups={{0,256,1,257},{2,258,3,259},{4,260,5,261},{6,262,7,263},{8,10,12,14},{2..., dimensions={0} | all-to-all | bytes 2097152 | tf_op jit(solution)/shard_map/all_to_all | solution.py:111
  63.8 2.6 %broadcast_in_dim.13 = bf16[4,4,128,1024]{3,2,1,0:T(8,128)(2,1)} broadcast(bf16[4,128,1024]{2,1,0:T(8,128)(2,1)S(1)} %all_to_all.16), dimensions={1,2,3} | broadcast | bytes 5242880 | tf_op jit(solution)/shard_map/broadcast_in_dim | solution.py:110
  66.4 0.0 copy-start.1
  66.4 0.0 copy-start.2
  66.4 0.0 copy-start.3
  66.4 5.0 %all-to-all-start.2 = ((bf16[4,4,128,1024]{3,2,1,0:T(8,128)(2,1)}), bf16[4,4,128,1024]{3,2,1,0:T(8,128)(2,1)}, u32[]{:S(2)}, u32[]{:S(2)}) async-start(bf16[4,4,128,1024]{3,2,1,0:T(8,128)(2,1)} %broadcast_in_dim.13), calls=%async_computation.2 | async-start | bytes 8388608 | tf_op jit(solution)/shard_map/all_to_all | solution.py:111
  71.4 0.0 copy-done.1
  71.4 0.6 reshape.82.gain
  72.0 0.0 copy-done.2
  72.0 0.0 copy-done.3
  72.0 0.6 broadcast_in_dim.14.bias
  72.6 0.7 add_select_fusion.table
  73.3 0.8 fusion
  74.0 25.1 %all-to-all-done.2 = bf16[4,4,128,1024]{3,2,1,0:T(8,128)(2,1)} async-done(((bf16[4,4,128,1024]{3,2,1,0:T(8,128)(2,1)}), bf16[4,4,128,1024]{3,2,1,0:T(8,128)(2,1)}, u32[]{:S(2)}, u32[]{:S(2)}) %all-to-all-start.2) | async-done | bytes 4194336 | tf_op jit(solution)/shard_map/all_to_all | solution.py:111
  99.2 0.0 all-gather.2.cloned.1.call-done.weights
  99.2 11.0 %project.1 = (bf16[2,128,512]{2,1,0:T(8,128)(2,1)}, bf16[2,128,128]{2,1,0:T(8,128)(2,1)}) custom-call(s32[2,8]{1,0:T(2,128)} %add_select_fusion.table, bf16[16,128,1024]{2,1,0:T(8,128)(2,1)} %bitcast.3.first.second, bf16[16,128,1024]{2,1,0:T(8,128)(2,1)} %bitcast.3.first.second, bf16[8,1,1024]{2,1,0:T(2,128)(2,1)} %reshape.82.gain, ...), custom_call_target="tpu_custom_call" | custom-call | tf_op jit(solution)/shard_map/project/pallas_call | solution.py:80
  (4 shorter events, 0.0 us)
Async XLA Ops:
  7.2 92.0 %all-gather.2.cloned.1.call-start = ((), (), s32[]{:S(2)}) async-start(), calls=%async_computation.3 | async-start | bytes 10813440 | tf_op jit(solution)/shard_map/all_gather | solution.py:119
  14.6 35.5 %copy-start = (bf16[1,128,1024]{2,1,0:T(8,128)(2,1)S(1)}, bf16[1,128,1024]{2,1,0:T(8,128)(2,1)}, u32[]{:S(2)}) copy-start(bf16[1,128,1024]{2,1,0:T(8,128)(2,1)} %param.8) | copy-start | bytes 786436
  66.4 5.0 %copy-start.1 = (bf16[8192]{0:T(1024)(128)(2,1)S(1)}, bf16[8192]{0:T(1024)(128)(2,1)}, u32[]{:S(2)}) copy-start(bf16[8192]{0:T(1024)(128)(2,1)} %param.9) | copy-start | bytes 49156
  66.4 5.7 %copy-start.2 = (bf16[512]{0:T(512)(128)(2,1)S(1)}, bf16[512]{0:T(512)(128)(2,1)}, u32[]{:S(2)}) copy-start(bf16[512]{0:T(512)(128)(2,1)} %param.12) | copy-start | bytes 3076
  66.4 5.7 %copy-start.3 = (bf16[128]{0:T(256)(128)(2,1)S(1)}, bf16[128]{0:T(256)(128)(2,1)}, u32[]{:S(2)}) copy-start(bf16[128]{0:T(256)(128)(2,1)} %param.13) | copy-start | bytes 772
  66.4 32.8 %all-to-all-start.2 = ((bf16[4,4,128,1024]{3,2,1,0:T(8,128)(2,1)}), bf16[4,4,128,1024]{3,2,1,0:T(8,128)(2,1)}, u32[]{:S(2)}, u32[]{:S(2)}) async-start(bf16[4,4,128,1024]{3,2,1,0:T(8,128)(2,1)} %broadcast_in_dim.13), calls=%async_computation.2 | async-start | bytes 8388608 | tf_op jit(solution)/shard_map/all_to_all | solution.py:111
Sparse Core Ops, SparseCore 0:
  10.1 78.4 all-gather.1
